TPU v7x, 32 devices: a whole 2x2x4 slice. The times are simulated.
32 devices in a mesh: owner: 8 (over z, y), rows: 4 (over x, core).
Axes of the slice: x: 2, y: 2, z: 4, core: 2. Of those that a mesh axis runs over, the one named last changes fastest.
Arguments:
- master_down: float32 [16, 6400, 4096], P('owner', None, 'rows'), may hold values from -0.109375 to 0.109375
- router_weight: float32 [4096, 16], P('rows', 'owner'), may hold values from -0.09375 to 0.09375
- router_gain: float32 [4096], P('rows'), may hold values from 0.25 to 1.75
Outputs:
- final_down: bfloat16 [16, 6400, 4096], P('owner', 'rows')
- scale_down: float32 [16, 6400], P('owner', 'rows')
- serve_router: bfloat16 [4096, 16], replicated
All inputs are finite; a program needn't handle non-finite values. Where the computation divides by a largest or mean magnitude, that divisor is 1e-20 or more.
Results may differ from a plain program's by a relative error of at most 0.001.
Values may be sent and summed in bfloat16 or wider, within the bound.
A program may use at most 192 MiB of HBM per device.

v0:
```python
import jax
import jax.numpy as jnp
from jax import lax
from jax.sharding import PartitionSpec as P

D_MODEL = 4096


def per_device(master_down, router_weight, router_gain):
    total_down = lax.psum(jnp.sum(jnp.abs(master_down), axis=2), "rows")
    scale_down = total_down / D_MODEL
    narrow_down = (master_down / jnp.expand_dims(scale_down, 2)).astype(jnp.bfloat16)
    final_down = lax.all_to_all(narrow_down, "rows", split_axis=1, concat_axis=2, tiled=True)
    scale_down = lax.dynamic_slice_in_dim(
        scale_down, lax.axis_index("rows") * final_down.shape[1], final_down.shape[1], axis=1
    )
    part_router = (router_weight * router_gain[:, None]).astype(jnp.bfloat16)
    row_router = lax.all_gather(part_router, "rows", axis=0, tiled=True)
    serve_router = lax.all_gather(row_router, "owner", axis=1, tiled=True)
    return (final_down, scale_down, serve_router)


def solution(mesh):
    return jax.shard_map(
        per_device,
        mesh=mesh,
        in_specs=(P("owner", None, "rows"), P("rows", "owner"), P("rows")),
        out_specs=(P("owner", "rows", None), P("owner", "rows"), P()),
        check_vma=False,
    )
```

profile of v0, /device:TPU:0, one launch (start us, length us, event | category | flops | bytes accessed | tf_op | source)
XLA Modules:
  0.0 506.3 jit_solution(15090514093543817720)
XLA Ops:
  0.6 17.0 %abs_reduce_fusion = f32[2,6400]{1,0:T(2,128)S(1)} fusion(f32[2,6400,1024]{2,1,0:T(8,128)} %param.3), kind=kLoop, calls=%fused_computation.1 | loop fusion | flops 26201600 | bytes 52480000 | tf_op jit(solution)/shard_map/reduce_sum | solution.py:10
  17.6 13.4 %psum.7 = f32[2,6400]{1,0:T(2,128)S(1)} all-reduce(f32[2,6400]{1,0:T(2,128)S(1)} %abs_reduce_fusion), channel_id=1, replica_groups=mesh['owner'=8,'rows'=4] {'rows'}, use_global_device_ids=true, to_apply=%region_1.0 | all-reduce | flops 12800 | bytes 102400 | tf_op jit(solution)/shard_map/psum | solution.py:10
  31.1 26.1 %divide_convert_fusion = bf16[2,6400,1024]{2,1,0:T(8,128)(2,1)} fusion(f32[2,6400,1024]{2,1,0:T(8,128)} %param.3, f32[2,6400]{1,0:T(2,128)S(1)} %broadcast_multiply_fusion), kind=kLoop, calls=%fused_computation | loop fusion | flops 26214400 | bytes 78694400 | tf_op jit(solution)/shard_map/convert_element_type | solution.py:12
  57.2 0.0 copy-start
  57.2 0.0 copy-start.1
  57.2 47.4 %copy.10 = bf16[2,6400,1024]{2,0,1:T(2,128)(2,1)} copy(bf16[2,6400,1024]{2,1,0:T(8,128)(2,1)} %divide_convert_fusion) | data formatting | bytes 52428800 | tf_op jit(solution)/shard_map/convert_element_type | solution.py:12
  104.6 8.6 %all-to-all-start = ((bf16[2,6400,1024]{2,0,1:T(2,128)(2,1)}), bf16[2,6400,1024]{2,0,1:T(2,128)(2,1)}, u32[]{:S(2)}, u32[]{:S(2)}) async-start(bf16[2,6400,1024]{2,0,1:T(2,128)(2,1)} %copy.10), calls=%async_computation | async-start | bytes 52428800 | tf_op jit(solution)/shard_map/all_to_all | solution.py:13
  113.2 0.0 copy-done
  113.2 0.0 copy-done.1
  113.2 285.0 %all_gather.6 = bf16[4096,2]{0,1:T(2,128)(2,1)S(1)} all-gather(bf16[1024,2]{0,1:T(2,128)(2,1)S(1)} %multiply_convert_fusion), channel_id=1, replica_groups=mesh['owner'=8,'rows'=4] {'rows'}, dimensions={0}, use_global_device_ids=true | all-gather | bytes 20480 | tf_op jit(solution)/shard_map/all_gather | solution.py:18
  398.2 30.9 %all-gather = bf16[8,2,4096]{2,1,0:T(2,128)(2,1)S(1)} all-gather(bf16[1,2,4096]{2,1,0:T(2,128)(2,1)S(1)} %bitcast.8), channel_id=1, replica_groups=mesh['owner'=8,'rows'=4] {'owner'}, dimensions={0}, use_global_device_ids=true | all-gather | bytes 147456 | tf_op jit(solution)/shard_map/all_gather | solution.py:19
  429.1 0.7 reshape.9
  429.8 0.7 constant_dynamic-slice_fusion
  430.5 0.0 all-to-all-done
  430.5 33.4 %copy.11 = bf16[2,1600,4,1024]{3,2,1,0:T(4,128)(2,1)} copy(bf16[2,1600,4,1024]{3,0,1,2:T(2,128)(2,1)} %bitcast.1) | data formatting | bytes 52428800 | tf_op jit(solution)/shard_map/all_to_all | solution.py:13
  463.9 42.5 %all_to_all.16 = bf16[2,1600,4096]{2,1,0:T(8,128)(2,1)} reshape(bf16[2,1600,4,1024]{3,2,1,0:T(4,128)(2,1)} %copy.11) | data formatting | bytes 52428800 | tf_op jit(solution)/shard_map/all_to_all | solution.py:13
  (2 shorter events, 0.0 us)
Async XLA Ops:
  57.2 56.0 %copy-start = (f32[1024,2]{0,1:T(2,128)S(1)}, f32[1024,2]{0,1:T(2,128)}, u32[]{:S(2)}) copy-start(f32[1024,2]{0,1:T(2,128)} %param.4) | copy-start | bytes 24580
  57.2 56.0 %copy-start.1 = (f32[1024]{0:T(1024)S(1)}, f32[1024]{0:T(1024)}, u32[]{:S(2)}) copy-start(f32[1024]{0:T(1024)} %param.5) | copy-start | bytes 12292
  104.6 325.9 %all-to-all-start = ((bf16[2,6400,1024]{2,0,1:T(2,128)(2,1)}), bf16[2,6400,1024]{2,0,1:T(2,128)(2,1)}, u32[]{:S(2)}, u32[]{:S(2)}) async-start(bf16[2,6400,1024]{2,0,1:T(2,128)(2,1)} %copy.10), calls=%async_computation | async-start | bytes 52428800 | tf_op jit(solution)/shard_map/all_to_all | solution.py:13
where the time goes:
time: 508 us; the launch traced here: 506 us
  blocking collectives  329 us (65%)
  local copies, waits for them, and re-layouts  125 us (25%)
  other arithmetic  43.2 us (9%)
  starting transfers between devices  8.59 us (2%)
    all_gather x1, blocking collectives, per_device(): row_router = lax.all_gather(part_router, 'rows', axis=0, tiled=True)  285 us
    all_to_all x2, local copies, waits for them, and re-layouts, per_device(): lax.all_to_all(narrow_down, 'rows', split_axis=1, concat_axis=2, tiled=True)  75.8 us
    convert_element_type x1, local copies, waits for them, and re-layouts, per_device(): (master_down / jnp.expand_dims(scale_down, 2)).astype(jnp.bfloat16)  47.4 us
    all_gather x1, blocking collectives, per_device(): serve_router = lax.all_gather(row_router, 'owner', axis=1, tiled=True)  30.9 us
    convert_element_type x1, other arithmetic, per_device(): (master_down / jnp.expand_dims(scale_down, 2)).astype(jnp.bfloat16)  26.1 us
    reduce_sum x1, other arithmetic, per_device(): total_down = lax.psum(jnp.sum(jnp.abs(master_down), axis=2), 'rows')  17 us
    psum x1, blocking collectives, per_device(): total_down = lax.psum(jnp.sum(jnp.abs(master_down), axis=2), 'rows')  13.4 us
  transfers between devices with their start and end apart: 1, of which 0 were waited for; matrix products, arithmetic and copies ran while one was open for 0% of the time, Pallas kernels for 0%

commit v1 on v0

v1 whole, which is shorter than its diff:
```python
import functools

import jax
import jax.numpy as jnp
from jax import lax
from jax.experimental import pallas as pl
from jax.experimental.pallas import tpu as pltpu
from jax.sharding import PartitionSpec as P

LANES = 128
SLOTS = 3


def rows_per_block(quota, n):
    fits = [r for r in range(16, quota + 1, 16) if quota % r == 0 and (n * r) % LANES == 0]
    small = [r for r in fits if r * n <= 1280 and r <= 160]
    return max(small) if small else (min(fits) if fits else quota)


def kernel(n, steps, first, per, x_ref, out_ref, scale_ref, fbuf, nbuf, acc, mine, peers,
           load_sem, send_sem, recv_sem, own_sem, sum_send, sum_recv):
    me = lax.axis_index("rows")
    rows, width = fbuf.shape[2], fbuf.shape[3]
    groups = width // LANES

    barrier = pltpu.get_barrier_semaphore()
    for d in range(1, n):
        pl.semaphore_signal(
            barrier, inc=1, device_id={"rows": lax.rem(me + d, n)},
            device_id_type=pl.DeviceIdType.MESH,
        )

    def load(t):
        slot = t % SLOTS
        return pltpu.make_async_copy(x_ref.at[t // per, :, t % per], fbuf.at[slot], load_sem.at[slot])

    def prefetch(lo, hi):
        for t in range(lo, min(lo + SLOTS - 1, hi)):
            load(t).start()

    def stream(lo, hi, body):
        def step(t, carry):
            @pl.when(t + SLOTS - 1 < hi)
            def _():
                load(t + SLOTS - 1).start()

            load(t).wait()
            body(t, t % SLOTS)
            return carry

        lax.fori_loop(lo, hi, step, 0)

    def add_up(t, slot):
        for j in range(n):
            part = jnp.abs(fbuf[slot, j, :, :LANES])
            for g in range(1, groups):
                part = part + jnp.abs(fbuf[slot, j, :, g * LANES:(g + 1) * LANES])
            acc[j * rows:(j + 1) * rows, :] = part
        mine[t] = jnp.sum(acc[...].T, axis=0, keepdims=True)

    def exchange(turn, lo, hi):
        return [
            pltpu.make_async_remote_copy(
                src_ref=mine.at[pl.ds(lo, hi - lo)],
                dst_ref=peers.at[d - 1, pl.ds(lo, hi - lo)],
                send_sem=sum_send.at[turn, d - 1],
                recv_sem=sum_recv.at[turn, d - 1],
                device_id={"rows": lax.rem(me + d, n)},
                device_id_type=pl.DeviceIdType.MESH,
            )
            for d in range(1, n)
        ]

    def block(t, d):
        there = lax.rem(me + d, n)
        return pltpu.make_async_remote_copy(
            src_ref=nbuf.at[t, there],
            dst_ref=out_ref.at[t // per, pl.ds(pl.multiple_of((t % per) * rows, rows), rows),
                               pl.ds(pl.multiple_of(me * width, width), width)],
            send_sem=send_sem.at[d - 1, t],
            recv_sem=recv_sem.at[d - 1, t],
            device_id={"rows": there},
            device_id_type=pl.DeviceIdType.MESH,
        )

    def own(t):
        return pltpu.make_async_copy(
            nbuf.at[t, me],
            out_ref.at[t // per, pl.ds(pl.multiple_of((t % per) * rows, rows), rows),
                       pl.ds(pl.multiple_of(me * width, width), width)],
            own_sem.at[t],
        )

    def send(t):
        for d in range(1, n):
            block(t, d).start()
        own(t).start()

    def narrow(t):
        total = mine[t]
        for d in range(1, n):
            total = total + peers[d - 1, t]
        scale = total / (n * width)
        scale_ref[t] = scale
        acc[...] = jnp.broadcast_to(1.0 / scale, (LANES, n * rows)).T

    def scale_and_send(lo):
        def body(t, slot):
            narrow(t)
            for j in range(n):
                inverse = acc[j * rows:(j + 1) * rows, :]
                for g in range(groups):
                    cut = slice(g * LANES, (g + 1) * LANES)
                    nbuf[t, j, :, cut] = (fbuf[slot, j, :, cut] * inverse).astype(jnp.bfloat16)

            @pl.when(t > lo)
            def _():
                send(t - 1)

        return body

    prefetch(0, first)
    stream(0, first, add_up)
    prefetch(0, first)
    pl.semaphore_wait(barrier, n - 1)
    sums = exchange(0, 0, first)
    for copy in sums:
        copy.start()
    for copy in sums:
        copy.wait()
    stream(0, first, scale_and_send(0))
    if first < steps:
        prefetch(first, steps)
        stream(first, steps, add_up)
        prefetch(first, steps)
        sums = exchange(1, first, steps)
        for copy in sums:
            copy.start()
        send(first - 1)
        for copy in sums:
            copy.wait()
        stream(first, steps, scale_and_send(first))
    send(steps - 1)

    def finish(t, carry):
        for d in range(1, n):
            block(t, d).wait()
        own(t).wait()
        return carry

    lax.fori_loop(0, steps, finish, 0)


def per_device(n, master_down, router_weight, router_gain):
    experts, height, width = master_down.shape
    quota = height // n
    rows = rows_per_block(quota, n)
    per = quota // rows
    steps = experts * per
    first = min(max(3, -(-steps // 8)), steps)
    cut = n * rows
    final_down, scales = pl.pallas_call(
        functools.partial(kernel, n, steps, first, per),
        out_shape=(
            jax.ShapeDtypeStruct((experts, quota, n * width), jnp.bfloat16),
            jax.ShapeDtypeStruct((steps, 1, cut), jnp.float32),
        ),
        in_specs=[pl.BlockSpec(memory_space=pl.ANY)],
        out_specs=(pl.BlockSpec(memory_space=pl.ANY), pl.BlockSpec(memory_space=pltpu.VMEM)),
        scratch_shapes=[
            pltpu.VMEM((SLOTS, n, rows, width), jnp.float32),
            pltpu.VMEM((steps, n, rows, width), jnp.bfloat16),
            pltpu.VMEM((cut, LANES), jnp.float32),
            pltpu.VMEM((steps, 1, cut), jnp.float32),
            pltpu.VMEM((n - 1, steps, 1, cut), jnp.float32),
            pltpu.SemaphoreType.DMA((SLOTS,)),
            pltpu.SemaphoreType.DMA((n - 1, steps)),
            pltpu.SemaphoreType.DMA((n - 1, steps)),
            pltpu.SemaphoreType.DMA((steps,)),
            pltpu.SemaphoreType.DMA((2, n - 1)),
            pltpu.SemaphoreType.DMA((2, n - 1)),
        ],
        compiler_params=pltpu.CompilerParams(
            collective_id=0, has_side_effects=True, vmem_limit_bytes=48 * 1024 * 1024,
        ),
    )(master_down.reshape(experts, n, per, rows, width))
    by_device = scales.reshape(experts, per, n, rows)
    scale_down = lax.dynamic_index_in_dim(by_device, lax.axis_index("rows"), axis=2, keepdims=False)
    scale_down = scale_down.reshape(experts, quota)

    part_router = (router_weight * router_gain[:, None]).astype(jnp.bfloat16)
    row_router = lax.all_gather(part_router, "rows", axis=0, tiled=True)
    serve_router = lax.all_gather(row_router, "owner", axis=1, tiled=True)
    return (final_down, scale_down, serve_router)


def solution(mesh):
    return jax.shard_map(
        functools.partial(per_device, mesh.shape["rows"]),
        mesh=mesh,
        in_specs=(P("owner", None, "rows"), P("rows", "owner"), P("rows")),
        out_specs=(P("owner", "rows", None), P("owner", "rows"), P()),
        check_vma=False,
    )
```

time: 508 us -> 354 us (0.70)
  Pallas kernels: 0 us -> 294 us
  blocking collectives: 329 us -> 36.4 us
  local copies, waits for them, and re-layouts: 125 us -> 23.2 us
  other arithmetic: 43.2 us -> 0.13 us
  starting transfers between devices: 8.59 us -> 0 us
    pallas_call x0 -> x1, Pallas kernels: none -> 294 us  [per_device(): pl.pallas_call(functools.partial(kernel, n, steps, first, per), out_shape...]
    all_gather x1, blocking collectives: 285 us -> 5.56 us  [per_device(): row_router = lax.all_gather(part_router, 'rows', axis=0, tiled=True)]
    all_to_all x2 -> x0, local copies, waits for them, and re-layouts: 75.8 us -> none  [per_device(): lax.all_to_all(narrow_down, 'rows', split_axis=1, concat_axis=2, tiled=True)]
    convert_element_type x1 -> x0, local copies, waits for them, and re-layouts: 47.4 us -> none  [per_device(): (master_down / jnp.expand_dims(scale_down, 2)).astype(jnp.bfloat16)]
    convert_element_type x1 -> x0, other arithmetic: 26.1 us -> none  [per_device(): (master_down / jnp.expand_dims(scale_down, 2)).astype(jnp.bfloat16)]
    unnamed x5 -> x6, local copies, waits for them, and re-layouts: 0.71 us -> 22.4 us
    reduce_sum x1 -> x0, other arithmetic: 17 us -> none  [per_device(): total_down = lax.psum(jnp.sum(jnp.abs(master_down), axis=2), 'rows')]
    psum x1 -> x0, blocking collectives: 13.4 us -> none  [per_device(): total_down = lax.psum(jnp.sum(jnp.abs(master_down), axis=2), 'rows')]
  transfers between devices with their start and end apart: 1 -> 0, of which waited for: 0 -> 0; matrix products, arithmetic and copies ran while one was open for 0% -> 0% of each run, Pallas kernels for 0% -> 0%
where the time goes in v1:
time: 354 us
  Pallas kernels  294 us (83%)
  blocking collectives  36.4 us (10%)
  local copies, waits for them, and re-layouts  23.2 us (7%)
    pallas_call x1, Pallas kernels, per_device(): pl.pallas_call(functools.partial(kernel, n, steps, first, per), out_shape...  294 us
    all_gather x1, blocking collectives, per_device(): serve_router = lax.all_gather(row_router, 'owner', axis=1, tiled=True)  30.9 us
    unnamed x6, local copies, waits for them, and re-layouts  22.4 us

profile of v1, /device:TPU:0, one launch (start us, length us, event | category | flops | bytes accessed | tf_op | source)
XLA Modules:
  0.0 354.0 jit_solution(1724076064255179669)
XLA Ops:
  0.6 0.0 copy-start
  0.6 0.0 copy-start.1
  0.7 293.5 %shard_map.58 = (bf16[2,1600,4096]{2,1,0:T(8,128)(2,1)}, f32[20,1,640]{2,1,0:T(1,128)S(1)}) custom-call(f32[2,4,10,160,1024]{4,3,2,1,0:T(8,128)} %bitcast.5), custom_call_target="tpu_custom_call" | custom-call | tf_op jit(solution)/shard_map/pallas_call | solution.py:162
  294.2 0.1 reduce
  294.3 0.1 reshape.18
  294.4 0.1 dynamic-slice_reduce_fusion
  294.5 0.7 reshape.19
  295.2 0.0 copy-done
  295.2 0.0 copy-done.1
  295.2 5.6 %all_gather.6 = bf16[4096,2]{0,1:T(2,128)(2,1)S(1)} all-gather(bf16[1024,2]{0,1:T(2,128)(2,1)S(1)} %multiply_convert_fusion), channel_id=1, replica_groups=mesh['owner'=8,'rows'=4] {'rows'}, dimensions={0}, use_global_device_ids=true | all-gather | bytes 20480 | tf_op jit(solution)/shard_map/all_gather | solution.py:192
  300.8 30.9 %all-gather = bf16[8,2,4096]{2,1,0:T(2,128)(2,1)S(1)} all-gather(bf16[1,2,4096]{2,1,0:T(2,128)(2,1)S(1)} %bitcast.7), channel_id=1, replica_groups=mesh['owner'=8,'rows'=4] {'owner'}, dimensions={0}, use_global_device_ids=true | all-gather | bytes 147456 | tf_op jit(solution)/shard_map/all_gather | solution.py:193
  331.6 0.7 reshape.21
  332.3 21.7 %copy.7 = bf16[2,1600,4096]{2,1,0:T(8,128)(2,1)} copy(bf16[2,1600,4096]{2,1,0:T(8,128)(2,1)} %get-tuple-element.10) | data formatting | bytes 52428800
  (1 shorter events, 0.0 us)
Async XLA Ops:
  0.6 294.6 %copy-start = (f32[1024,2]{0,1:T(2,128)S(1)}, f32[1024,2]{0,1:T(2,128)}, u32[]{:S(2)}) copy-start(f32[1024,2]{0,1:T(2,128)} %param.4) | copy-start | bytes 24580
  0.6 294.5 %copy-start.1 = (f32[1024]{0:T(1024)S(1)}, f32[1024]{0:T(1024)}, u32[]{:S(2)}) copy-start(f32[1024]{0:T(1024)} %param.5) | copy-start | bytes 12292

commit v2 on v1

--- a/solution.py
+++ b/solution.py
@@ -17,9 +17,11 @@
     return max(small) if small else (min(fits) if fits else quota)
 
 
-def kernel(n, steps, first, per, x_ref, out_ref, scale_ref, fbuf, nbuf, acc, mine, peers,
-           load_sem, send_sem, recv_sem, own_sem, sum_send, sum_recv):
+def kernel(n, owners, steps, first, per, x_ref, weight_ref, gain_ref, out_ref, scale_ref, router_ref, fbuf, nbuf, acc, mine, peers,
+           strip, load_sem, send_sem, recv_sem, own_sem, sum_send, sum_recv, strip_send, strip_recv,
+           router_send, router_recv):
     me = lax.axis_index("rows")
+    home = lax.axis_index("owner")
     rows, width = fbuf.shape[2], fbuf.shape[3]
     groups = width // LANES
 
@@ -27,6 +29,32 @@
     for d in range(1, n):
         pl.semaphore_signal(
             barrier, inc=1, device_id={"rows": lax.rem(me + d, n)},
+            device_id_type=pl.DeviceIdType.MESH,
+        )
+    for d in range(1, owners):
+        pl.semaphore_signal(
+            barrier, inc=1, device_id={"owner": lax.rem(home + d, owners)},
+            device_id_type=pl.DeviceIdType.MESH,
+        )
+    strip[me] = (weight_ref[...] * gain_ref[...]).astype(jnp.bfloat16)
+
+    def row_strip(d):
+        return pltpu.make_async_remote_copy(
+            src_ref=strip.at[me],
+            dst_ref=strip.at[me],
+            send_sem=strip_send.at[d - 1],
+            recv_sem=strip_recv.at[d - 1],
+            device_id={"rows": lax.rem(me + d, n)},
+            device_id_type=pl.DeviceIdType.MESH,
+        )
+
+    def owner_strips(d):
+        return pltpu.make_async_remote_copy(
+            src_ref=strip,
+            dst_ref=router_ref.at[home],
+            send_sem=router_send.at[d - 1],
+            recv_sem=router_recv.at[d - 1],
+            device_id={"owner": lax.rem(home + d, owners)},
             device_id_type=pl.DeviceIdType.MESH,
         )
 
@@ -101,7 +129,7 @@
         for d in range(1, n):
             total = total + peers[d - 1, t]
         scale = total / (n * width)
-        scale_ref[t] = scale
+        scale_ref[pl.ds(t, 1), :] = scale
         acc[...] = jnp.broadcast_to(1.0 / scale, (LANES, n * rows)).T
 
     def scale_and_send(lo):
@@ -122,13 +150,20 @@
     prefetch(0, first)
     stream(0, first, add_up)
     prefetch(0, first)
-    pl.semaphore_wait(barrier, n - 1)
+    pl.semaphore_wait(barrier, n - 1 + owners - 1)
     sums = exchange(0, 0, first)
     for copy in sums:
         copy.start()
+    for d in range(1, n):
+        row_strip(d).start()
     for copy in sums:
         copy.wait()
     stream(0, first, scale_and_send(0))
+    for d in range(1, n):
+        row_strip(d).wait()
+    for d in range(1, owners):
+        owner_strips(d).start()
+    router_ref[home] = strip[...]
     if first < steps:
         prefetch(first, steps)
         stream(first, steps, add_up)
@@ -149,9 +184,11 @@
         return carry
 
     lax.fori_loop(0, steps, finish, 0)
-
-
-def per_device(n, master_down, router_weight, router_gain):
+    for d in range(1, owners):
+        owner_strips(d).wait()
+
+
+def per_device(n, owners, master_down, router_weight, router_gain):
     experts, height, width = master_down.shape
     quota = height // n
     rows = rows_per_block(quota, n)
@@ -159,44 +196,57 @@
     steps = experts * per
     first = min(max(3, -(-steps // 8)), steps)
     cut = n * rows
-    final_down, scales = pl.pallas_call(
-        functools.partial(kernel, n, steps, first, per),
+    depth, mine = router_weight.shape
+    final_down, scales, strips = pl.pallas_call(
+        functools.partial(kernel, n, owners, steps, first, per),
         out_shape=(
             jax.ShapeDtypeStruct((experts, quota, n * width), jnp.bfloat16),
-            jax.ShapeDtypeStruct((steps, 1, cut), jnp.float32),
+            jax.ShapeDtypeStruct((steps, cut), jnp.float32),
+            jax.ShapeDtypeStruct((owners, n, mine, depth), jnp.bfloat16),
         ),
-        in_specs=[pl.BlockSpec(memory_space=pl.ANY)],
-        out_specs=(pl.BlockSpec(memory_space=pl.ANY), pl.BlockSpec(memory_space=pltpu.VMEM)),
+        in_specs=[
+            pl.BlockSpec(memory_space=pl.ANY),
+            pl.BlockSpec(memory_space=pltpu.VMEM),
+            pl.BlockSpec(memory_space=pltpu.VMEM),
+        ],
+        out_specs=(
+            pl.BlockSpec(memory_space=pl.ANY),
+            pl.BlockSpec(memory_space=pltpu.VMEM),
+            pl.BlockSpec(memory_space=pltpu.VMEM),
+        ),
         scratch_shapes=[
             pltpu.VMEM((SLOTS, n, rows, width), jnp.float32),
             pltpu.VMEM((steps, n, rows, width), jnp.bfloat16),
             pltpu.VMEM((cut, LANES), jnp.float32),
             pltpu.VMEM((steps, 1, cut), jnp.float32),
             pltpu.VMEM((n - 1, steps, 1, cut), jnp.float32),
+            pltpu.VMEM((n, mine, depth), jnp.bfloat16),
             pltpu.SemaphoreType.DMA((SLOTS,)),
             pltpu.SemaphoreType.DMA((n - 1, steps)),
             pltpu.SemaphoreType.DMA((n - 1, steps)),
             pltpu.SemaphoreType.DMA((steps,)),
             pltpu.SemaphoreType.DMA((2, n - 1)),
             pltpu.SemaphoreType.DMA((2, n - 1)),
+            pltpu.SemaphoreType.DMA((n - 1,)),
+            pltpu.SemaphoreType.DMA((n - 1,)),
+            pltpu.SemaphoreType.DMA((owners - 1,)),
+            pltpu.SemaphoreType.DMA((owners - 1,)),
         ],
         compiler_params=pltpu.CompilerParams(
             collective_id=0, has_side_effects=True, vmem_limit_bytes=48 * 1024 * 1024,
         ),
-    )(master_down.reshape(experts, n, per, rows, width))
+    )(master_down.reshape(experts, n, per, rows, width), router_weight.T, router_gain[None, :])
     by_device = scales.reshape(experts, per, n, rows)
     scale_down = lax.dynamic_index_in_dim(by_device, lax.axis_index("rows"), axis=2, keepdims=False)
     scale_down = scale_down.reshape(experts, quota)
 
-    part_router = (router_weight * router_gain[:, None]).astype(jnp.bfloat16)
-    row_router = lax.all_gather(part_router, "rows", axis=0, tiled=True)
-    serve_router = lax.all_gather(row_router, "owner", axis=1, tiled=True)
+    serve_router = strips.transpose(0, 2, 1, 3).reshape(owners * mine, n * depth).T
     return (final_down, scale_down, serve_router)
 
 
 def solution(mesh):
     return jax.shard_map(
-        functools.partial(per_device, mesh.shape["rows"]),
+        functools.partial(per_device, mesh.shape["rows"], mesh.shape["owner"]),
         mesh=mesh,
         in_specs=(P("owner", None, "rows"), P("rows", "owner"), P("rows")),
         out_specs=(P("owner", "rows", None), P("owner", "rows"), P()),

time: 354 us -> 321 us (0.907)
  blocking collectives: 36.4 us -> 0 us
    all_gather x2 -> x0, blocking collectives: 36.4 us -> none  [the longest x1 30.9 us: per_device(): serve_router = lax.all_gather(row_router, 'owner', axis=1, tiled=True)]
where the time goes in v2:
time: 321 us; the launch traced here: 320 us
  Pallas kernels  295 us (92%)
  local copies, waits for them, and re-layouts  24.6 us (8%)
    pallas_call x1, Pallas kernels, per_device(): pl.pallas_call(functools.partial(kernel, n, owners, steps, first, per), o...  295 us
    unnamed x6, local copies, waits for them, and re-layouts  23.7 us

profile of v2, /device:TPU:0, one launch (start us, length us, event | category | flops | bytes accessed | tf_op | source)
XLA Modules:
  0.0 320.0 jit_solution(8879563055414213338)
XLA Ops:
  0.6 0.0 copy-start
  0.6 0.7 copy-done
  1.3 0.0 copy-start.1
  1.3 0.7 copy-done.1
  2.0 294.6 %shard_map.58 = (bf16[2,1600,4096]{2,1,0:T(8,128)(2,1)}, f32[20,640]{1,0:T(8,128)S(1)}, bf16[8,4,2,1024]{3,2,1,0:T(2,128)(2,1)S(1)}) custom-call(f32[2,4,10,160,1024]{4,3,2,1,0:T(8,128)} %bitcast.12, f32[2,1024]{1,0:T(2,128)S(1)} %bitcast.10, f32[1,1024]{1,0:T(1,128)S(1)} %bitcast.11), custom_call_target="tpu_custom_call" | custom-call | tf_op jit(solution)/shard_map/pallas_call | solution.py:200
  296.7 0.1 reshape.20
  296.8 0.1 dynamic-slice_reduce_fusion
  296.9 0.7 reshape.21
  297.6 0.1 copy.6
  297.6 0.7 copy.7
  298.3 21.7 %copy.9 = bf16[2,1600,4096]{2,1,0:T(8,128)(2,1)} copy(bf16[2,1600,4096]{2,1,0:T(8,128)(2,1)} %get-tuple-element.12) | data formatting | bytes 52428800
Async XLA Ops:
  0.6 0.7 copy-start
  1.3 0.7 copy-start.1
